TPU v7x, 32 devices: a 4x4x1 block of a 4x4x8 slice. The times are simulated.
32 devices in a mesh: dp: 1 (over z), wy: 4 (over y), wx: 8 (over x, core).
Axes of the slice: x: 4, y: 4, z: 1, core: 2. Of those that a mesh axis runs over, the one named last changes fastest.
The devices are a block of a 4x4x8 slice.
Arguments:
- x_tokens: bfloat16 [32, 128, 2048], P(('dp', 'wy', 'wx'))
- gamma_ln: float32 [2, 2048], replicated
- w_q: bfloat16 [2, 2048, 2048], P(None, 'wx', 'wy')
- w_kv: bfloat16 [2, 2048, 2, 128], P(None, 'wx')
- w_gu: bfloat16 [2, 2048, 2, 8192], P(None, 'wx', None, 'wy')
- w_o: bfloat16 [2, 2048, 2048], P(None, 'wy', 'wx')
- w_d: bfloat16 [2, 8192, 2048], P(None, 'wy', 'wx')
Outputs:
- output 1: bfloat16 [32, 128, 2048], P(('dp', 'wy', 'wx'))
- output 2: bfloat16 [2, 32, 128, 128], P(None, ('dp', 'wy', 'wx'))
- output 3: bfloat16 [2, 32, 128, 128], P(None, ('dp', 'wy', 'wx'))
All inputs are finite; a program needn't handle non-finite values.
Results may differ from a plain program's by a relative error of at most 0.0157459.
Values are sent between devices in bfloat16 or wider.
A program may use at most 768 MiB of HBM per device.

v0:
```python
import functools

import jax
import jax.numpy as jnp
import numpy as np
from jax import lax
from jax.experimental import pallas as pl
from jax.experimental.pallas import tpu as pltpu
from jax.sharding import PartitionSpec as P

LN_EPS = 1e-6
ROPE_BASE = 10000.0
CORES = 2
GU_CHUNKS = 4
HALVES = 2
BF, F32 = jnp.bfloat16, jnp.float32

L0, R1, SIDES, OWN_CHIP, FAR_CHIP = range(5)
A_L, A_R, A_TOP, A_BOT, A_SIB = range(5)


def rope_tables(seq_len, head_dim):
    inv_freq = np.float32(ROPE_BASE) ** (-2.0 * np.arange(head_dim // 2, dtype=np.float32) / head_dim).astype(np.float32)
    angles = np.arange(seq_len, dtype=np.float32)[:, None] * inv_freq[None, :]
    cos_tab, sin_tab = np.cos(angles.astype(np.float64)), np.sin(angles.astype(np.float64))
    return (np.concatenate([cos_tab, cos_tab], axis=-1).astype(np.float32),
            np.concatenate([-sin_tab, sin_tab], axis=-1).astype(np.float32))


def layers_kernel(dims, gamma_in, cos_in, sin_in, x_ref, wq, wkv, wgu, wo, wd,
                  y_out, k_out, v_out,
                  bq, bkv, bgu, bod, hbuf, qbuf, kvbuf, ombuf, part, rs0, rs1, rs2, resid,
                  gu_raw, kv_raw, gu_stage, kv_stage, gamma_ref, cos_ref, sin_ref, raw_sem,
                  w_send, w_recv, c_recv, kvw_send, kvw_recv, a_send, a_recv, kv_send, kv_recv, r_send, r_recv, out_sem):
    layers, n_x, n_y, seq, head_dim, rows, width = dims
    heads = wo.shape[1] // CORES // head_dim
    hid = wd.shape[1] // CORES
    o_rows = wo.shape[1] // CORES
    q_cols = heads * head_dim
    g_cols = hid // GU_CHUNKS
    n_prompts = CORES * n_y
    toks = n_prompts * seq
    keep = n_y * seq
    tile = toks // 4

    wx = lax.axis_index('wx')
    y = lax.axis_index('wy')
    x, c = wx // CORES, wx % CORES
    xr, xl, xo = (x + 1) % n_x, (x + n_x - 1) % n_x, (x + 2) % n_x
    yr, yl, yo = (y + 1) % n_y, (y + n_y - 1) % n_y, (y + 2) % n_y
    sibling = {'wx': x * CORES + 1 - c}
    right_y, left_y = {'wy': yr}, {'wy': yl}

    def at_x(chip, core):
        return {'wx': chip * CORES + core}

    n_gu = layers * GU_CHUNKS
    tables = ((gamma_in, gamma_ref), (cos_in, cos_ref), (sin_in, sin_ref))
    kv_rows = rows // n_y

    def gu_load(g, core):
        cols = pl.ds(core * hid + (g % GU_CHUNKS) * g_cols, g_cols)
        return pltpu.make_async_copy(wgu.at[g // GU_CHUNKS, :, :, cols], gu_raw.at[g % 2, core], raw_sem.at[g % 2])

    def kv_load(l):
        mine = pl.ds(pl.multiple_of(y * kv_rows, kv_rows), kv_rows)
        return pltpu.make_async_copy(wkv.at[l, mine], kv_raw.at[l], raw_sem.at[3 + l])

    def x_load(i):
        return pltpu.make_async_copy(x_ref.at[0, :, pl.ds(i * width, width)], resid.at[i], raw_sem.at[2])

    barrier = pltpu.get_barrier_semaphore()
    peers = [sibling, right_y, left_y] + [at_x(chip, core) for chip in (xr, xl) for core in range(CORES)]
    for peer in peers:
        pl.semaphore_signal(barrier, inc=1, device_id=peer, device_id_type=pl.DeviceIdType.MESH)
    kv_load(0).start()
    for core in range(CORES):
        gu_load(0, core).start()
    for core in range(CORES):
        gu_load(1, core).start()
    for i in range(resid.shape[0]):
        x_load(i).start()
    for n, (table, held) in enumerate(tables):
        pltpu.make_async_copy(table, held, raw_sem.at[3 + layers + n]).start()
    for l in range(1, layers):
        kv_load(l).start()
    pl.semaphore_wait(barrier, len(peers))

    def remote(src, dst, send_sem, recv_sem, peer):
        return pltpu.make_async_remote_copy(src_ref=src, dst_ref=dst, send_sem=send_sem, recv_sem=recv_sem,
                                            device_id=peer, device_id_type=pl.DeviceIdType.MESH)

    def wait_in(ref, recv_sem, send_sem):
        remote(ref, ref, send_sem, recv_sem, sibling).wait_recv()

    def wait_out(ref, recv_sem, send_sem):
        remote(ref, ref, send_sem, recv_sem, sibling).wait_send()

    order = ('q', 'kv', 'gu', 'od')
    pieces = []
    n_blocks = n_outs = 0
    for l in range(layers):
        pieces.append([('q', l, 0, n_blocks), ('kv', l, 0, n_blocks + 1)])
        n_blocks += 2
        for j in range(GU_CHUNKS):
            pieces.append([('gu', l, j, n_blocks)])
            n_blocks += 1
        for hh in range(HALVES):
            pieces.append([('od', l, hh, n_outs)])
            n_outs += 1
    per_layer = len(pieces) // layers
    issue_after = [[p + 2] for p in range(len(pieces))]
    tail = len(pieces) - HALVES
    issue_after[tail - 2] = []
    issue_after[tail - 1] = [tail + hh for hh in range(HALVES)]
    issue_after[tail:] = [[] for _ in range(HALVES)]

    def sources(block, core):
        kind, l, j, _ = block
        if kind == 'q':
            return [wq.at[l, :, pl.ds(pl.multiple_of(core * q_cols, q_cols), q_cols)]]
        if kind == 'kv':
            return [kv_stage.at[l, core]]
        if kind == 'gu':
            return [gu_stage.at[l, j, core]]
        cols = pl.ds(j * width, width)
        return [wo.at[l, pl.ds(pl.multiple_of(core * o_rows, o_rows), o_rows), cols],
                wd.at[l, pl.ds(pl.multiple_of(core * hid, hid), hid), cols]]

    def landing(block, chip, core):
        kind, l, j, _ = block
        if kind == 'kv':
            return bkv.at[l, chip * CORES + core, y]
        if kind == 'od':
            return bod.at[l, j, chip, :, pl.ds(pl.multiple_of(core * width, width), width)]
        row = pl.ds(pl.multiple_of((chip * CORES + core) * rows, rows), rows)
        return bq.at[l, row] if kind == 'q' else bgu.at[l, j, row]

    def landings(block):
        here = landing(block, x, c)
        return [here.at[pl.ds(0, o_rows)], here.at[pl.ds(o_rows, hid)]] if block[0] == 'od' else [here]

    def received(block, how):
        return c_recv.at[block[3], how] if block[0] == 'od' else w_recv.at[block[3], how]

    def prepare_kv(l):
        kv_load(l).wait()
        for core in range(CORES):
            kv_stage[l, core] = kv_raw[l, :, core, :]

    def prepare(p):
        if p >= len(pieces) or pieces[p][0][0] != 'gu':
            return
        _, l, j, _ = pieces[p][0]
        g = l * GU_CHUNKS + j
        step_rows = rows // 4
        pltpu.make_async_copy(gu_raw.at[g % 2], gu_raw.at[g % 2], raw_sem.at[g % 2]).wait()
        for core in range(CORES):
            def step(i, carry):
                at = pl.ds(pl.multiple_of(i * step_rows, step_rows), step_rows)
                for which in range(2):
                    gu_stage[l, j, core, at, which * g_cols:(which + 1) * g_cols] = gu_raw[g % 2, core, at, which, :]
                return carry
            lax.fori_loop(0, 4, step, 0)
            if g + 2 < n_gu:
                gu_load(g + 2, core).start()

    def issue_own(p, only=None):
        if p >= len(pieces):
            return
        for block in pieces[p] if only is None else [pieces[p][only]]:
            sent = w_send.at[order.index(block[0])]
            side = [SIDES * c, SIDES - c]
            near = OWN_CHIP if block[0] == 'od' else SIDES
            for core in range(CORES):
                for src, dst in zip(sources(block, core), landings(block)):
                    remote(src, dst, sent, received(block, side[0]), at_x(xr, core)).start()
                    remote(src, dst, sent, received(block, side[1]), at_x(xl, core)).start()
            for src, dst in zip(sources(block, 1 - c), landings(block)):
                remote(src, dst, sent, received(block, near), sibling).start()
            for src, dst in zip(sources(block, c), landings(block)):
                pltpu.make_async_copy(src, dst, received(block, near)).start()

    def wait_block(block, how):
        kind, l, j, _ = block
        if how in (L0, R1):
            ref = landing(block, xl, 0) if how == L0 else landing(block, xr, 1)
        elif kind == 'od':
            ref = bod.at[l, j, {SIDES: xl, OWN_CHIP: x, FAR_CHIP: xo}[how]]
        else:
            others = n_x * CORES - 2
            ref = bkv.at[l, pl.ds(0, others), y] if kind == 'kv' else (
                bq.at[l, pl.ds(0, others * rows)] if kind == 'q' else bgu.at[l, j, pl.ds(0, others * rows)])
        wait_in(ref, received(block, how), w_send.at[0])

    done = [0]

    def comm(p):
        if p >= len(pieces):
            return
        assert p == done[0]
        done[0] = p + 1
        for block in pieces[p]:
            far = FAR_CHIP if block[0] == 'od' else SIDES
            wait_block(block, L0)
            from_left = landing(block, xl, 0)
            remote(from_left, from_left, w_send.at[order.index(block[0])], received(block, far), at_x(xr, c)).start()
            wait_block(block, R1)
            from_right = landing(block, xr, 1)
            remote(from_right, from_right, w_send.at[order.index(block[0])], received(block, far), at_x(xl, c)).start()
        for later in issue_after[p]:
            issue_own(later)
        prepare(p + 3)

    def wait_piece(p, hows):
        for block in pieces[p]:
            for how in hows:
                wait_block(block, how)

    def drain_weights():
        n_src = n_x * CORES
        for n, ref in enumerate((bq.at[:, pl.ds(0, (n_src - 1) * rows)], bkv.at[:, pl.ds(0, n_src - 1), 0],
                                 bgu.at[:, :, pl.ds(0, (n_src - 1) * rows)],
                                 bod.at[:, :, :, pl.ds(0, (o_rows + hid) // n_src * (n_src - 1))])):
            wait_out(ref, w_recv.at[0, 0], w_send.at[n])

    def kv_quarter(l, yy, half=None):
        n_src = n_x * CORES
        return bkv.at[l, pl.ds(0 if half is None else half * (n_src // 2), n_src if half is None else n_src // 2), yy]

    def kvw_copy(l, ref, kind, peer):
        remote(ref, ref, kvw_send.at[l], kvw_recv.at[l, kind], peer).start()

    def kvw_send_own(l):
        kvw_copy(l, kv_quarter(l, y), A_L, right_y)
        kvw_copy(l, kv_quarter(l, y), A_R, left_y)

    def kvw_forward(l):
        wait_in(kv_quarter(l, yl), kvw_recv.at[l, A_L], kvw_send.at[l])
        kvw_copy(l, kv_quarter(l, yl, 0), A_TOP, right_y)
        wait_in(kv_quarter(l, yr), kvw_recv.at[l, A_R], kvw_send.at[l])
        kvw_copy(l, kv_quarter(l, yr, 1), A_BOT, left_y)

    def kvw_finish(l):
        wait_in(kv_quarter(l, yo, 0), kvw_recv.at[l, A_TOP], kvw_send.at[l])
        wait_in(kv_quarter(l, yo, 1), kvw_recv.at[l, A_BOT], kvw_send.at[l])
        wait_out(bkv.at[l, :, pl.ds(0, n_y - 1)], kvw_recv.at[l, A_L], kvw_send.at[l])

    def prompt(slot, part_of=None):
        if part_of is None:
            return hbuf.at[pl.ds(pl.multiple_of(slot * seq, seq), seq)]
        half = seq // 2
        return hbuf.at[pl.ds(pl.multiple_of(slot * seq + part_of * half, half), half)]

    def a_copy(l, src, dst, kind, peer):
        remote(src, dst, a_send.at[l], a_recv.at[l, kind], peer).start()

    def a_wait(l, ref, kind):
        wait_in(ref, a_recv.at[l, kind], a_send.at[l])

    def gather_send(l):
        a_copy(l, prompt(y), prompt(y), A_L, right_y)
        a_copy(l, prompt(y), prompt(y), A_R, left_y)
        a_copy(l, prompt(y), prompt(n_y + y), A_SIB, sibling)

    def gather_forward(l):
        a_wait(l, prompt(yl), A_L)
        a_copy(l, prompt(yl, 0), prompt(yl, 0), A_TOP, right_y)
        a_copy(l, prompt(yl), prompt(n_y + yl), A_SIB, sibling)
        a_wait(l, prompt(yr), A_R)
        a_copy(l, prompt(yr, 1), prompt(yr, 1), A_BOT, left_y)
        a_copy(l, prompt(yr), prompt(n_y + yr), A_SIB, sibling)

    def gather_share(l):
        a_wait(l, prompt(yo, 0), A_TOP)
        a_copy(l, prompt(yo, 0), prompt(n_y + yo, 0), A_SIB, sibling)
        a_wait(l, prompt(yo, 1), A_BOT)
        a_copy(l, prompt(yo, 1), prompt(n_y + yo, 1), A_SIB, sibling)

    def gather_finish(l):
        a_wait(l, hbuf.at[pl.ds(keep, keep)], A_SIB)

    def gather_drain(l):
        wait_out(hbuf.at[pl.ds(0, 7 * seq)], a_recv.at[l, A_L], a_send.at[l])

    n_res = resid.shape[0]
    d_model = n_res * width

    def norm_own(l):
        total = jnp.zeros((seq, 1), F32)
        for i in range(n_res):
            total += jnp.sum(resid[i].astype(F32), axis=-1, keepdims=True)
        mean = total / d_model
        square = jnp.zeros((seq, 1), F32)
        for i in range(n_res):
            centered = resid[i].astype(F32) - mean
            square += jnp.sum(centered * centered, axis=-1, keepdims=True)
        scale = lax.rsqrt(square / d_model + LN_EPS)
        own = pl.ds(pl.multiple_of(y * seq, seq), seq)
        for i in range(n_res):
            value = (resid[i].astype(F32) - mean) * scale * gamma_ref[l:l + 1, i * width:(i + 1) * width]
            hbuf[own, i * width:(i + 1) * width] = value.astype(BF)

    def rotate(value):
        value = value.astype(F32)
        cos_all = jnp.concatenate([cos_ref[...]] * (tile // seq), axis=0)
        sin_all = jnp.concatenate([sin_ref[...]] * (tile // seq), axis=0)
        return (value * cos_all + pltpu.roll(value, head_dim // 2, 1) * sin_all).astype(BF)

    def tiles(body, n=4, size=tile):
        def step(i, carry):
            body(pl.multiple_of(i * size, size))
            return carry
        lax.fori_loop(0, n, step, 0)

    def project_q(l):
        def body(start):
            at = pl.ds(start, tile)
            acc = jnp.dot(hbuf[at, :], bq[l], preferred_element_type=F32).astype(BF)
            for n in range(heads):
                qbuf[at, n * head_dim:(n + 1) * head_dim] = rotate(acc[:, n * head_dim:(n + 1) * head_dim])
        tiles(body)

    def project_kv(l):
        def body(start):
            at = pl.ds(start, tile)
            weights = bkv[l].reshape(d_model, head_dim)
            kv = jnp.dot(hbuf[at, :], weights, preferred_element_type=F32).astype(BF)
            kvbuf[c, at, :] = jnp.where(c == 0, rotate(kv), kv)
        tiles(body)

    def kv_refs(lo):
        return kvbuf.at[c, pl.ds(lo * keep, keep)]

    def kv_exchange(l):
        for lo in range(2):
            remote(kv_refs(lo), kv_refs(1 - lo), kv_send.at[l], kv_recv.at[l], sibling).start()

    def kv_outs(l):
        own = pl.ds(pl.multiple_of(y * seq, seq), seq)
        return [pltpu.make_async_copy(kvbuf.at[0, own], k_out.at[l, 0], out_sem.at[l]),
                pltpu.make_async_copy(kvbuf.at[1, own], v_out.at[l, 0], out_sem.at[l])]

    def kv_finish(l):
        wait_in(kvbuf.at[1 - c], kv_recv.at[l], kv_send.at[l])
        for copy in kv_outs(l):
            copy.start()

    def kv_drain(l):
        wait_out(kvbuf.at[c], kv_recv.at[l], kv_send.at[l])
        both = kvbuf.at[0, pl.ds(0, 2 * seq)]
        pltpu.make_async_copy(both, both, out_sem.at[l]).wait()

    def attend():
        score_scale = head_dim ** -0.5
        allowed = lax.broadcasted_iota(jnp.int32, (seq, seq), 0) >= lax.broadcasted_iota(jnp.int32, (seq, seq), 1)

        def body(start):
            at = pl.ds(start, seq)
            key, val = kvbuf[0, at, :], kvbuf[1, at, :]
            for n in range(heads):
                query = qbuf[at, n * head_dim:(n + 1) * head_dim]
                scores = lax.dot_general(query, key, (((1,), (1,)), ((), ())), preferred_element_type=F32) * score_scale
                scores = jnp.where(allowed, scores, -jnp.inf)
                weights = jnp.exp(scores - jnp.max(scores, axis=-1, keepdims=True))
                probs = (weights / jnp.sum(weights, axis=-1, keepdims=True)).astype(BF)
                ombuf[at, n * head_dim:(n + 1) * head_dim] = jnp.dot(probs, val, preferred_element_type=F32).astype(BF)
        tiles(body, n_prompts, seq)

    def gate_up(l, j):
        def body(start):
            at = pl.ds(start, tile)
            acc = jnp.dot(hbuf[at, :], bgu[l, j], preferred_element_type=F32).astype(BF).astype(F32)
            ombuf[at, q_cols + j * g_cols:q_cols + (j + 1) * g_cols] = (jax.nn.silu(acc[:, :g_cols]) * acc[:, g_cols:]).astype(BF)
        tiles(body)

    chips = [x, xl, xr, xo]
    half_w = width

    def chunk(b, hh):
        return b * HALVES + hh

    def project_out(l, b, hh):
        k = chunk(b, hh)

        def step(i, carry):
            at = pl.ds(pl.multiple_of((1 - i) * keep, keep), keep)
            part[k, at, :] = jnp.dot(ombuf[at, :], bod[l, hh, chips[b]], preferred_element_type=F32)

            @pl.when(i == 0)
            def _():
                remote(part.at[k, pl.ds(keep, keep)], rs0.at[k], r_send.at[0], r_recv.at[k, 0], sibling).start()
            return carry
        lax.fori_loop(0, 2, step, 0)

    def of_chip_half(k, yy, side):
        return part.at[k, pl.ds(pl.multiple_of(yy * seq, seq), seq), pl.ds(side * half_w, half_w)]

    def send_near(k, target, side, half, peer):
        remote(of_chip_half(k, target, half), rs2.at[k, side, :, pl.ds(half * half_w, half_w)],
               r_send.at[2], r_recv.at[k, 3], peer).start()

    def reduce_cores(b, hh):
        k = chunk(b, hh)
        wait_in(rs0.at[k], r_recv.at[k, 0], r_send.at[0])
        part[k, 0:keep, :] += rs0[k]
        remote(of_chip_half(k, yo, 0), rs1.at[k, 0], r_send.at[1], r_recv.at[k, 1], right_y).start()
        remote(of_chip_half(k, yo, 1), rs1.at[k, 1], r_send.at[1], r_recv.at[k, 2], left_y).start()
        send_near(k, yr, 0, 1, right_y)
        send_near(k, yl, 1, 0, left_y)

    def reduce_far(b, hh):
        k = chunk(b, hh)
        for side, target, peer in ((0, yr, right_y), (1, yl, left_y)):
            wait_in(rs1.at[k, side], r_recv.at[k, 1 + side], r_send.at[1])
            at = pl.ds(pl.multiple_of(target * seq, seq), seq)
            part[k, at, side * half_w:(side + 1) * half_w] += rs1[k, side]
            send_near(k, target, side, side, peer)

    def out_copy(i):
        return pltpu.make_async_copy(resid.at[i], y_out.at[0, :, pl.ds(pl.multiple_of(i * width, width), width)],
                                     out_sem.at[layers])

    def reduce_last(l, b, hh):
        k = chunk(b, hh)
        wait_in(rs2.at[k], r_recv.at[k, 3], r_send.at[2])
        own = pl.ds(pl.multiple_of(y * seq, seq), seq)
        total = part[k, own, :] + rs2[k, 0] + rs2[k, 1]
        for core in range(CORES):
            i = (chips[b] * CORES + core) * HALVES + hh
            resid[i] = (resid[i].astype(F32) + total[:, core * width:(core + 1) * width]).astype(BF)
            if l == layers - 1:
                out_copy(i).start()

    def reduce_drain():
        for n, ref in enumerate((rs0, rs1, rs2)):
            wait_out(ref, r_recv.at[0, 0], r_send.at[n])

    issue_own(0, 0)
    for l in range(layers):
        prepare_kv(l)
    prepare(1)
    issue_own(0, 1)
    issue_own(1)
    prepare(2)
    pltpu.make_async_copy(resid, resid, raw_sem.at[2]).wait()
    for n, (table, held) in enumerate(tables):
        pltpu.make_async_copy(table, held, raw_sem.at[3 + layers + n]).wait()
    norm_own(0)
    gather_send(0)
    comm(0)
    gather_forward(0)
    gather_share(0)
    gather_finish(0)
    OWN, LEFT, RIGHT, FAR = range(4)
    rest = (SIDES,)
    for l in range(layers):
        base = l * per_layer
        last = l == layers - 1

        def ahead(p):
            while done[0] <= p:
                comm(done[0])

        ahead(base + 1)
        if l == 0:
            wait_piece(base, rest)
            kvw_send_own(l)
        project_q(l)
        ahead(base + 2)
        if l == 0:
            kvw_forward(l)
        wait_piece(base + 1, rest)
        gate_up(l, 0)
        kvw_finish(l)
        project_kv(l)
        kv_exchange(l)
        for j in range(1, GU_CHUNKS):
            ahead(base + 1 + j if last and j == GU_CHUNKS - 1 else base + 2 + j)
            wait_piece(base + 1 + j, rest)
            gate_up(l, j)
            if j == 1:
                kv_finish(l)
                attend()
        gather_drain(l)
        kv_drain(l)
        c0, c1 = base + 1 + GU_CHUNKS, base + 2 + GU_CHUNKS
        wait_piece(c0, (OWN_CHIP,))
        project_out(l, OWN, 0)
        wait_piece(c1, (OWN_CHIP,))
        project_out(l, OWN, 1)
        reduce_cores(OWN, 0)
        reduce_cores(OWN, 1)
        reduce_far(OWN, 0)
        ahead(c0)
        wait_piece(c0, (SIDES,))
        project_out(l, LEFT, 0)
        reduce_far(OWN, 1)
        project_out(l, RIGHT, 0)
        reduce_cores(LEFT, 0)
        reduce_cores(RIGHT, 0)
        reduce_last(l, OWN, 0)
        reduce_far(LEFT, 0)
        comm(c1)
        wait_piece(c1, (SIDES,))
        project_out(l, LEFT, 1)
        reduce_far(RIGHT, 0)
        reduce_last(l, OWN, 1)
        project_out(l, RIGHT, 1)
        reduce_cores(LEFT, 1)
        reduce_cores(RIGHT, 1)
        wait_piece(c0, (FAR_CHIP,))
        project_out(l, FAR, 0)
        reduce_last(l, LEFT, 0)
        reduce_far(LEFT, 1)
        reduce_far(RIGHT, 1)
        reduce_cores(FAR, 0)
        if not last:
            comm(c1 + 1)
        wait_piece(c1, (FAR_CHIP,))
        project_out(l, FAR, 1)
        reduce_far(FAR, 0)
        reduce_cores(FAR, 1)
        reduce_last(l, RIGHT, 0)
        reduce_last(l, LEFT, 1)
        reduce_last(l, RIGHT, 1)
        reduce_far(FAR, 1)
        reduce_last(l, FAR, 0)
        reduce_last(l, FAR, 1)
        reduce_drain()
        if not last:
            norm_own(l + 1)
            comm(c1 + 2)
            gather_send(l + 1)
            wait_piece(base + per_layer, rest)
            kvw_send_own(l + 1)
            gather_forward(l + 1)
            comm(c1 + 3)
            gather_share(l + 1)
            kvw_forward(l + 1)
            gather_finish(l + 1)
    drain_weights()
    pltpu.make_async_copy(resid, resid, out_sem.at[layers]).wait()


def take_over(y_in, k_in, v_in, y_out, k_out, v_out, y_held, k_held, v_held, sems):
    half = y_in.shape[1] // 2
    top, bottom = pl.ds(0, half), pl.ds(half, half)
    moves = [(y_in.at[0, top], y_held.at[top], y_out.at[0, top]), (y_in.at[0, bottom], y_held.at[bottom], y_out.at[0, bottom]),
             (k_in, k_held, k_out), (v_in, v_held, v_out)]
    loads = [pltpu.make_async_copy(src, held, sems.at[0, n]) for n, (src, held, _) in enumerate(moves)]
    stores = [pltpu.make_async_copy(held, dst, sems.at[1, n]) for n, (_, held, dst) in enumerate(moves)]
    for load in loads:
        load.start()
    for load, store in zip(loads, stores):
        load.wait()
        store.start()
    for store in stores:
        store.wait()


def run_layers(mesh_sizes, x_tokens, gamma_ln, w_q, w_kv, w_gu, w_o, w_d):
    n_x, n_y = mesh_sizes['wx'] // CORES, mesh_sizes['wy']
    assert n_x == 4 and n_y == 4 and x_tokens.shape[0] == 1
    layers, rows, q_loc = w_q.shape
    seq, d_model = x_tokens.shape[1:]
    head_dim = w_kv.shape[-1]
    hid_loc = w_gu.shape[-1]
    hid = hid_loc // CORES
    g_cols = hid // GU_CHUNKS
    q_cols = q_loc // CORES
    width = rows // HALVES
    toks = CORES * n_y * seq
    n_chunks = n_x * HALVES
    n_res = d_model // width
    cos_all, sin_all = rope_tables(seq, head_dim)
    dma = pltpu.SemaphoreType.DMA
    anywhere = pl.BlockSpec(memory_space=pl.ANY)
    cache = jax.ShapeDtypeStruct((layers, 1, seq, head_dim), BF)
    results = pl.pallas_call(
        functools.partial(layers_kernel, (layers, n_x, n_y, seq, head_dim, rows, width)),
        out_shape=(jax.ShapeDtypeStruct(x_tokens.shape, BF), cache, cache),
        in_specs=[anywhere] * 9,
        out_specs=(anywhere,) * 3,
        scratch_shapes=[
            pltpu.VMEM((layers, d_model, q_cols), BF),
            pltpu.VMEM((layers, n_x * CORES, n_y, rows // n_y, head_dim), BF),
            pltpu.VMEM((layers, GU_CHUNKS, d_model, 2 * g_cols), BF),
            pltpu.VMEM((layers, HALVES, n_x, q_cols + hid, CORES * width), BF),
            pltpu.VMEM((toks, d_model), BF),
            pltpu.VMEM((toks, q_cols), BF),
            pltpu.VMEM((2, toks, head_dim), BF),
            pltpu.VMEM((toks, q_cols + hid), BF),
            pltpu.VMEM((n_chunks, toks, CORES * width), F32),
            pltpu.VMEM((n_chunks, toks // CORES, CORES * width), F32),
            pltpu.VMEM((n_chunks, 2, seq, width), F32),
            pltpu.VMEM((n_chunks, 2, seq, CORES * width), F32),
            pltpu.VMEM((n_res, seq, width), BF),
            pltpu.VMEM((2, CORES, rows, 2, g_cols), BF),
            pltpu.VMEM((layers, rows // n_y, 2, head_dim), BF),
            pltpu.VMEM((layers, GU_CHUNKS, CORES, rows, 2 * g_cols), BF),
            pltpu.VMEM((layers, 2, rows // n_y, head_dim), BF),
            pltpu.VMEM(gamma_ln.shape, F32), pltpu.VMEM(cos_all.shape, F32), pltpu.VMEM(sin_all.shape, F32),
            dma((6 + layers,)),
            dma((4,)), dma((layers * (2 + GU_CHUNKS), 3)), dma((layers * HALVES, 5)),
            dma((layers,)), dma((layers, 4)),
            dma((layers,)), dma((layers, 5)),
            dma((layers,)), dma((layers,)),
            dma((3,)), dma((n_chunks, 4)),
            dma((layers + 1,)),
        ],
        compiler_params=pltpu.CompilerParams(collective_id=0, has_side_effects=True, vmem_limit_bytes=67043328),
    )(gamma_ln, cos_all, sin_all, x_tokens, w_q, w_kv, w_gu, w_o, w_d)
    shapes = [jax.ShapeDtypeStruct(r.shape, r.dtype) for r in results]
    return pl.pallas_call(
        take_over, out_shape=shapes, in_specs=[anywhere] * 3, out_specs=[anywhere] * 3,
        scratch_shapes=[pltpu.VMEM((seq, d_model), BF), pltpu.VMEM(cache.shape, BF), pltpu.VMEM(cache.shape, BF), dma((2, 4))],
    )(*results)


def solution(mesh):
    batch_axes = ('dp', 'wy', 'wx')
    in_specs = (P(batch_axes), P(), P(None, 'wx', 'wy'), P(None, 'wx'), P(None, 'wx', None, 'wy'), P(None, 'wy', 'wx'), P(None, 'wy', 'wx'))
    out_specs = (P(batch_axes), P(None, batch_axes), P(None, batch_axes))
    sizes = dict(mesh.shape)
    return jax.shard_map(functools.partial(run_layers, sizes), mesh=mesh, in_specs=in_specs, out_specs=out_specs, check_vma=False)
```

profile of v0, /device:TPU:97, one launch (start us, length us, event | category | flops | bytes accessed | tf_op | source)
XLA Modules:
  0.0 260.5 jit_solution(2589720753028565139)
XLA Ops:
  0.6 257.9 %shard_map.112 = (bf16[1,128,2048]{2,1,0:T(8,128)(2,1)}, bf16[2,1,128,128]{3,2,1,0:T(8,128)(2,1)}, bf16[2,1,128,128]{3,2,1,0:T(8,128)(2,1)}) custom-call(f32[2,2048]{1,0:T(2,128)} %gamma_in.1, f32[128,128]{1,0:T(8,128)} %constant.4.clone.cos_in, f32[128,128]{1,0:T(8,128)} %constant.5.clone.sin_in, bf16[1,128,2048]{2,1,0:T(8,128)(2,1)} %x_ref.1, ...), custom_call_target="tpu_custom_call" | custom-call | tf_op jit(solution)/shard_map/pallas_call | solution.py:580
  258.5 1.8 shard_map.113
where the time goes:
time: 261 us
  Pallas kernels  260 us (100%)
    pallas_call x1, Pallas kernels, run_layers(): pl.pallas_call(functools.partial(layers_kernel, (layers, n_x, n_y, seq, h...  258 us

commit v1 on v0

--- a/solution.py
+++ b/solution.py
@@ -41,7 +41,8 @@
     n_prompts = CORES * n_y
     toks = n_prompts * seq
     keep = n_y * seq
-    tile = toks // 4
+    tile = toks // 2
+    pair = keep // 2
 
     wx = lax.axis_index('wx')
     y = lax.axis_index('wy')
@@ -307,7 +308,7 @@
         sin_all = jnp.concatenate([sin_ref[...]] * (tile // seq), axis=0)
         return (value * cos_all + pltpu.roll(value, head_dim // 2, 1) * sin_all).astype(BF)
 
-    def tiles(body, n=4, size=tile):
+    def tiles(body, n=2, size=tile):
         def step(i, carry):
             body(pl.multiple_of(i * size, size))
             return carry
@@ -380,6 +381,9 @@
     def chunk(b, hh):
         return b * HALVES + hh
 
+    def pair_rows(n):
+        return pl.multiple_of((yo // 2 + n) % 2 * pair, pair)
+
     def project_out(l, b, hh):
         k = chunk(b, hh)
 
@@ -389,7 +393,10 @@
 
             @pl.when(i == 0)
             def _():
-                remote(part.at[k, pl.ds(keep, keep)], rs0.at[k], r_send.at[0], r_recv.at[k, 0], sibling).start()
+                for n in range(2):
+                    rows_at = pair_rows(n)
+                    remote(part.at[k, pl.ds(pl.multiple_of(keep + rows_at, pair), pair)],
+                           rs0.at[k, pl.ds(rows_at, pair)], r_send.at[0], r_recv.at[k, 4 * n], sibling).start()
             return carry
         lax.fori_loop(0, 2, step, 0)
 
@@ -402,10 +409,14 @@
 
     def reduce_cores(b, hh):
         k = chunk(b, hh)
-        wait_in(rs0.at[k], r_recv.at[k, 0], r_send.at[0])
-        part[k, 0:keep, :] += rs0[k]
+        at = pl.ds(pair_rows(0), pair)
+        wait_in(rs0.at[k, at], r_recv.at[k, 0], r_send.at[0])
+        part[k, at, :] += rs0[k, at, :]
         remote(of_chip_half(k, yo, 0), rs1.at[k, 0], r_send.at[1], r_recv.at[k, 1], right_y).start()
         remote(of_chip_half(k, yo, 1), rs1.at[k, 1], r_send.at[1], r_recv.at[k, 2], left_y).start()
+        at = pl.ds(pair_rows(1), pair)
+        wait_in(rs0.at[k, at], r_recv.at[k, 4], r_send.at[0])
+        part[k, at, :] += rs0[k, at, :]
         send_near(k, yr, 0, 1, right_y)
         send_near(k, yl, 1, 0, left_y)
 
@@ -606,7 +617,7 @@
             dma((layers,)), dma((layers, 4)),
             dma((layers,)), dma((layers, 5)),
             dma((layers,)), dma((layers,)),
-            dma((3,)), dma((n_chunks, 4)),
+            dma((3,)), dma((n_chunks, 5)),
             dma((layers + 1,)),
         ],
         compiler_params=pltpu.CompilerParams(collective_id=0, has_side_effects=True, vmem_limit_bytes=67043328),

time: 261 us -> 260 us (level)
  no operation moved by 1% of the time
where the time goes in v1:
time: 260 us
  Pallas kernels  259 us (100%)
    pallas_call x1, Pallas kernels, run_layers(): pl.pallas_call(functools.partial(layers_kernel, (layers, n_x, n_y, seq, h...  257 us

profile of v1, /device:TPU:97, one launch (start us, length us, event | category | flops | bytes accessed | tf_op | source)
XLA Modules:
  0.0 260.0 jit_solution(16957951472552072849)
XLA Ops:
  0.6 257.3 %shard_map.112 = (bf16[1,128,2048]{2,1,0:T(8,128)(2,1)}, bf16[2,1,128,128]{3,2,1,0:T(8,128)(2,1)}, bf16[2,1,128,128]{3,2,1,0:T(8,128)(2,1)}) custom-call(f32[2,2048]{1,0:T(2,128)} %gamma_in.1, f32[128,128]{1,0:T(8,128)} %constant.4.clone.cos_in, f32[128,128]{1,0:T(8,128)} %constant.5.clone.sin_in, bf16[1,128,2048]{2,1,0:T(8,128)(2,1)} %x_ref.1, ...), custom_call_target="tpu_custom_call" | custom-call | tf_op jit(solution)/shard_map/pallas_call | solution.py:591
  258.0 1.8 shard_map.113

commit v2 on v1

--- a/solution.py
+++ b/solution.py
@@ -503,19 +503,19 @@
         reduce_cores(OWN, 0)
         reduce_cores(OWN, 1)
         reduce_far(OWN, 0)
+        reduce_far(OWN, 1)
         ahead(c0)
         wait_piece(c0, (SIDES,))
         project_out(l, LEFT, 0)
-        reduce_far(OWN, 1)
         project_out(l, RIGHT, 0)
         reduce_cores(LEFT, 0)
         reduce_cores(RIGHT, 0)
         reduce_last(l, OWN, 0)
         reduce_far(LEFT, 0)
+        reduce_far(RIGHT, 0)
         comm(c1)
         wait_piece(c1, (SIDES,))
         project_out(l, LEFT, 1)
-        reduce_far(RIGHT, 0)
         reduce_last(l, OWN, 1)
         project_out(l, RIGHT, 1)
         reduce_cores(LEFT, 1)

time: 260 us -> 261 us (level)
  no operation moved by 1% of the time
where the time goes in v2:
time: 261 us; the launch traced here: 260 us
  Pallas kernels  259 us (99%)
    pallas_call x1, Pallas kernels, run_layers(): pl.pallas_call(functools.partial(layers_kernel, (layers, n_x, n_y, seq, h...  257 us

profile of v2, /device:TPU:97, one launch (start us, length us, event | category | flops | bytes accessed | tf_op | source)
XLA Modules:
  0.0 259.9 jit_solution(10234974686250377526)
XLA Ops:
  0.6 257.3 %shard_map.112 = (bf16[1,128,2048]{2,1,0:T(8,128)(2,1)}, bf16[2,1,128,128]{3,2,1,0:T(8,128)(2,1)}, bf16[2,1,128,128]{3,2,1,0:T(8,128)(2,1)}) custom-call(f32[2,2048]{1,0:T(2,128)} %gamma_in.1, f32[128,128]{1,0:T(8,128)} %constant.4.clone.cos_in, f32[128,128]{1,0:T(8,128)} %constant.5.clone.sin_in, bf16[1,128,2048]{2,1,0:T(8,128)(2,1)} %x_ref.1, ...), custom_call_target="tpu_custom_call" | custom-call | tf_op jit(solution)/shard_map/pallas_call | solution.py:591
  257.9 1.8 shard_map.113
